TPU v7x, 128 devices: a whole 4x4x4 slice. The times are simulated.
128 devices in a mesh: data: 1, model: 128 (over z, y, x, core).
Axes of the slice: x: 4, y: 4, z: 4, core: 2. Of those that a mesh axis runs over, the one named last changes fastest.
Arguments:
- queries: bfloat16 [32, 2048], P('data')
- w_head: bfloat16 [2048, 32000], P(None, 'model')
- ds_keys: bfloat16 [262144, 2048], P('model')
- ds_tokens: int32 [262144], P('model')
- temperature: float32 [1], replicated
- mix_weight: float32 [1], replicated
Outputs:
- output: float32 [32, 32000], P('data', 'model')
All inputs are finite; a program needn't handle non-finite values.
Results may differ from a plain program's by a relative error of at most 0.001.
Values are sent between devices in bfloat16 or wider.
A program may use at most 1 GiB of HBM per device.

v0:
```python
import jax
import jax.numpy as jnp
from jax import lax
from jax.sharding import PartitionSpec as P


def solution(mesh):
    group_size = mesh.shape["model"]

    def local_step(queries, w_shard, key_shard, tok_shard, value_a11, mix_weight):
        row_count = queries.shape[0]
        vocab_size = w_shard.shape[1] * group_size
        cross_dot = jnp.einsum("bd,nd->bn", queries, key_shard, preferred_element_type=jnp.float32)
        key_sq = jnp.sum(jnp.square(key_shard.astype(jnp.float32)), axis=1)
        scores = (2.0 * cross_dot - key_sq[None, :]) / value_a11[0]
        row_max = lax.pmax(jnp.max(scores, axis=1), "model")
        weights = jnp.exp(scores - row_max[:, None])
        row_total = lax.psum(jnp.sum(weights, axis=1), "model")
        local_hist = jnp.zeros((row_count, vocab_size), jnp.float32).at[:, tok_shard].add(weights)
        histogram = lax.psum_scatter(local_hist, "model", scatter_dimension=1, tiled=True)
        logits = jnp.dot(queries, w_shard, preferred_element_type=jnp.float32)
        lm_max = lax.pmax(jnp.max(logits, axis=1), "model")
        lm_exp = jnp.exp(logits - lm_max[:, None])
        lm_total = lax.psum(jnp.sum(lm_exp, axis=1), "model")
        mix_value = mix_weight[0]
        p_knn = histogram / row_total[:, None]
        p_lm = lm_exp / lm_total[:, None]
        return jnp.log(mix_value * p_knn + (1.0 - mix_value) * p_lm)

    return jax.shard_map(
        local_step,
        mesh=mesh,
        in_specs=(P("data", None), P(None, "model"), P("model", None), P("model"), P(), P()),
        out_specs=P("data", "model"),
        check_vma=False,
    )
```

profile of v0, /device:TPU:1, one launch (start us, length us, event | category | flops | bytes accessed | tf_op | source)
XLA Modules:
  0.0 279.4 jit_solution(10133865281772181169)
XLA Ops:
  6.5 0.0 copy-start
  6.5 0.0 all-reduce.5.cloned.1.call-start
  6.5 0.8 compare_select_fusion
  8.0 5.1 %multiply_reduce_fusion = f32[2048]{0:T(1024)S(1)} fusion(bf16[2048,2048]{1,0:T(8,128)(2,1)} %param.8), kind=kLoop, calls=%fused_computation.1 | loop fusion | flops 12580864 | bytes 8396800 | tf_op jit(solution)/shard_map/reduce_sum | solution.py:14
  13.1 0.0 copy-done
  13.1 1.3 fusion.11
  14.4 6.1 %fusion.10 = (f32[32]{0:T(128)S(1)}, f32[32,2048]{1,0:T(8,128)S(1)}) fusion(f32[]{:T(128)} %bitcast.10, f32[2048]{0:T(1024)S(1)} %multiply_reduce_fusion, bf16[32,2048]{1,0:T(8,128)(2,1)} %param.6, bf16[2048,2048]{1,0:T(8,128)(2,1)} %param.8), kind=kOutput, calls=%fused_computation.17 | convolution fusion | flops 268697568 | bytes 8790148 | tf_op jit(solution)/shard_map/bd,nd->bn/dot_general | solution.py:13
  20.5 68.7 %all-reduce.2 = (f32[32]{0:T(128)S(1)}, f32[32]{0:T(128)S(1)}) all-reduce(f32[32]{0:T(128)S(1)} %get-tuple-element.11, f32[32]{0:T(128)S(1)} %get-tuple-element.13), channel_id=1, replica_groups=mesh['data'=1,'model'=128] {'model'}, use_global_device_ids=true, to_apply=%region_2.0 | all-reduce | flops 64 | bytes 512 | tf_op jit(solution)/shard_map/pmax | solution.py:16
  89.2 0.2 fusion.4
  89.4 0.3 copy.9
  89.8 18.1 %scatter_custom_fusion = f32[32,32000]{0,1:T(8,128)} fusion(s32[2048]{0:T(1024)S(1)} %compare_select_fusion, f32[2048,32]{1,0:T(8,128)S(1)} %copy.9, f32[]{:T(128)} %constant.6.clone.1), kind=kCustom, calls=%fused_computation.2 | custom fusion | flops 65536 | bytes 4096004 | tf_op jit(solution)/shard_map/scatter-add | solution.py:19
  107.9 11.4 %copy.10 = f32[32,32000]{1,0:T(8,128)} copy(f32[32,32000]{0,1:T(8,128)} %scatter_custom_fusion) | data formatting | bytes 8192000 | tf_op jit(solution)/shard_map/scatter-add | solution.py:19
  119.2 0.0 all-reduce.5.cloned.1.call-update
  119.3 0.2 fusion.9
  119.4 62.8 %all-reduce.1 = (f32[32]{0:T(128)S(1)}, f32[32]{0:T(128)S(1)}) all-reduce(f32[32]{0:T(128)S(1)} %fusion.9, f32[32]{0:T(128)S(1)} %get-tuple-element.9), channel_id=1, replica_groups=mesh['data'=1,'model'=128] {'model'}, use_global_device_ids=true, to_apply=%region_10.0 | all-reduce | flops 64 | bytes 512 | tf_op jit(solution)/shard_map/psum | solution.py:24
  182.9 88.2 %all-reduce.5.cloned.1.call-done = f32[32,32000]{1,0:T(8,128)} async-done(((f32[32,32000]{1,0:T(8,128)}), f32[32,32000]{1,0:T(8,128)}) %all-reduce.5.cloned.1.call-update) | async-done | bytes 4096016
  271.1 1.5 fusion.8
Async XLA Ops:
  6.5 6.5 %copy-start = (bf16[2048,250]{1,0:T(8,128)(2,1)S(1)}, bf16[2048,250]{1,0:T(8,128)(2,1)}, u32[]{:S(2)}) copy-start(bf16[2048,250]{1,0:T(8,128)(2,1)} %param.7) | copy-start | bytes 3072004
  6.5 264.5 %all-reduce.5.cloned.1.call-start = ((), (), s32[]{:S(2)}) async-start(), calls=%async_computation | async-start | bytes 8192000
Sparse Core Ops, SparseCore 0:
  119.4 151.6 all-reduce.4
where the time goes:
time: 280 us; the launch traced here: 279 us
  blocking collectives  131 us (47%)
  waiting for transfers between devices  88.2 us (32%)
  other arithmetic  25.9 us (9%)
  between operations  14.7 us (5%)
  local copies, waits for them, and re-layouts  11.7 us (4%)
  matrix products  7.44 us (3%)
    unnamed x2, waiting for transfers between devices  88.2 us
    pmax x1, blocking collectives, local_step(): row_max = lax.pmax(jnp.max(scores, axis=1), 'model')  68.7 us
    psum x1, blocking collectives, local_step(): lm_total = lax.psum(jnp.sum(lm_exp, axis=1), 'model')  62.8 us
    scatter-add x1, other arithmetic, local_step(): jnp.zeros((row_count, vocab_size), jnp.float32).at[:, tok_shard]  18.1 us
    scatter-add x1, local copies, waits for them, and re-layouts, local_step(): jnp.zeros((row_count, vocab_size), jnp.float32).at[:, tok_shard]  11.4 us
    dot_general x1, matrix products, local_step(): jnp.einsum('bd,nd->bn', queries, key_shard, preferred_element_type=jnp.fl...  6.15 us
  transfers between devices with their start and end apart: 1, of which 1 were waited for; matrix products, arithmetic and copies ran while one was open for 0% of the time, Pallas kernels for 0%

commit v1 on v0

v1 whole, which is shorter than its diff:
```python
import functools

import jax
import jax.numpy as jnp
from jax import lax
from jax.experimental import pallas as pl
from jax.experimental.pallas import tpu as pltpu
from jax.sharding import PartitionSpec as P

MESH = pl.DeviceIdType.MESH
F32 = jnp.float32
BF16 = jnp.bfloat16
LANES = 128
ROWS = 11
CAP = 4 * ROWS
STAT = 64
COUNT = 48
EMPTY = 255.0


def _iota(shape, dim):
    return lax.broadcasted_iota(jnp.int32, shape, dim).astype(F32)


def _split3(x):
    hi = x.astype(BF16)
    rest = x - hi.astype(F32)
    mid = rest.astype(BF16)
    low = (rest - mid.astype(F32)).astype(BF16)
    return hi, mid, low


def _kernel(
    n_dev, rnd_ref, tau_ref, mix_ref, q_hbm, w_hbm, key_hbm, tok_hbm,
    p_ref, plm_ref, cnt_ref,
    q_ref, w_ref, key_ref, tok_ref, hot_ref, pack_ref, rhs_ref, s_ref, mask_ref, send, recv, x_ref,
    in_sem, key_sem, send_sem, recv_sem,
):
    me = lax.axis_index("model")
    n_rows, dim = q_ref.shape
    n_keys = key_ref.shape[0]
    v_loc = w_ref.shape[1]
    n_blk = n_keys // LANES
    n_chunk = key_sem.shape[0]
    step = n_keys // n_chunk

    loads = [
        pltpu.make_async_copy(src, dst, in_sem.at[i])
        for i, (src, dst) in enumerate([(tok_hbm, tok_ref), (q_hbm, q_ref), (w_hbm, w_ref)])
    ]
    loads += [
        pltpu.make_async_copy(key_hbm.at[pl.ds(i * step, step)], key_ref.at[pl.ds(i * step, step)], key_sem.at[i])
        for i in range(n_chunk)
    ]
    for load in loads:
        load.start()

    barrier = pltpu.get_barrier_semaphore()

    def greet(o, carry):
        pl.semaphore_signal(barrier, inc=1, device_id={"model": lax.rem(me + o, n_dev)}, device_id_type=MESH)
        return carry

    lax.fori_loop(1, n_dev, greet, 0)

    loads[0].wait()
    tok = tok_ref[...].astype(F32)
    owner = jnp.floor((tok + 0.5) * (1.0 / v_loc))
    place = tok - owner * v_loc + 1.0
    sub = _iota((LANES, LANES), 0)
    lane = _iota((LANES, LANES), 1)
    for c in range(n_blk):
        hot_ref[:, c * LANES : (c + 1) * LANES] = jnp.where(sub == owner[c : c + 1, :], 1.0, 0.0).astype(BF16)
    ones = jnp.ones((LANES, LANES), BF16)
    upper = jnp.where(sub <= lane, 1.0, 0.0).astype(BF16)
    tri = jnp.concatenate([upper, ones], axis=1)
    hot_rows = jnp.concatenate([hot_ref[:, c * LANES : (c + 1) * LANES] for c in range(n_blk)], axis=0)
    ranks = jnp.dot(hot_rows, tri, preferred_element_type=F32)
    before = jnp.zeros((LANES, LANES), F32)
    first = rnd_ref[0].astype(F32) * float(CAP) + 1.0
    for c in range(n_blk):
        part = ranks[c * LANES : (c + 1) * LANES]
        mine = sub == owner[c : c + 1, :]
        slot = jnp.sum(jnp.where(mine, part[:, :LANES] + before, 0.0), axis=0, keepdims=True) - first
        before = before + part[:, LANES:]
        slot = jnp.where((slot >= 0.0) & (slot < float(CAP)), slot, EMPTY)
        diag = sub == lane
        slot_col = jnp.dot(jnp.where(diag, slot, 0.0).astype(BF16), ones, preferred_element_type=F32)
        place_col = jnp.dot(
            jnp.where(diag, place[c : c + 1, :], 0.0).astype(BF16), ones, preferred_element_type=F32
        )
        rows = pl.ds(c * LANES, LANES)
        rhs_ref[rows, 0:LANES] = jnp.where(slot_col == lane, place_col, 0.0).astype(BF16)
        mask_ref[rows, :] = slot_col - 4.0 * jnp.floor(slot_col * 0.25)
        code = owner[c : c + 1, :] + LANES * jnp.floor(slot * 0.25)
        for r in range(ROWS):
            pack_ref[r * LANES : (r + 1) * LANES, c * LANES : (c + 1) * LANES] = jnp.where(
                sub + float(r * LANES) == code, 1.0, 0.0
            ).astype(BF16)
    meta = jnp.dot(hot_ref[...], rhs_ref[:, 0:LANES], preferred_element_type=F32)
    biggest = jnp.max(before, axis=0, keepdims=True)

    loads[1].wait()
    loads[2].wait()
    q = q_ref[...]
    logits = jnp.dot(q, w_ref[...], preferred_element_type=F32)
    lm_max = jnp.max(logits, axis=1, keepdims=True)
    lm_lse = lm_max + jnp.log(jnp.sum(jnp.exp(logits - lm_max), axis=1, keepdims=True))
    q_sub = _iota((n_rows, LANES), 0)
    q_lane = _iota((n_rows, LANES), 1)
    lse_row = jnp.sum(jnp.where(q_lane == q_sub + float(STAT + 32), lm_lse, 0.0), axis=0, keepdims=True)

    q4 = jnp.concatenate([q, q, q, q], axis=0)
    inv_tau = 1.0 / jnp.full((1, LANES), tau_ref[0], F32)
    top = jnp.full((1, LANES), -jnp.inf, F32)
    for i in range(n_chunk):
        loads[3 + i].wait()
        rows = pl.ds(i * step, step)
        dots = lax.dot_general(key_ref[rows, :], q4, (((1,), (1,)), ((), ())), preferred_element_type=F32)
        sq = jnp.zeros((step, LANES), F32)
        for t in range(dim // LANES):
            k = key_ref[rows, t * LANES : (t + 1) * LANES].astype(F32)
            sq = sq + k * k
        s = (2.0 * dots - jnp.sum(sq, axis=1, keepdims=True)) * inv_tau
        s_ref[rows, :] = s
        top = jnp.maximum(top, jnp.max(s, axis=0, keepdims=True))
    total = jnp.zeros((1, LANES), F32)
    for i in range(n_chunk):
        rows = pl.ds(i * step, step)
        e = jnp.exp(s_ref[rows, :] - top)
        s_ref[rows, :] = e
        total = total + jnp.sum(e, axis=0, keepdims=True)
    scale = 1.0 / total
    knn_lse = top + jnp.log(total)
    group = jnp.floor(_iota((step, LANES), 1) * (1.0 / 32.0))
    for i in range(n_chunk):
        rows = pl.ds(i * step, step)
        parts = _split3(jnp.where(mask_ref[rows, :] == group, s_ref[rows, :] * scale, 0.0))
        for k in range(3):
            rhs_ref[rows, k * LANES : (k + 1) * LANES] = parts[k]

    packed = jnp.dot(pack_ref[...], rhs_ref[...], preferred_element_type=F32)
    packed = packed[:, :LANES] + packed[:, LANES : 2 * LANES] + packed[:, 2 * LANES :]
    for r in range(ROWS):
        send[r] = packed[r * LANES : (r + 1) * LANES]
    row_lane = _iota((1, LANES), 1)
    stats = jnp.where((row_lane >= float(STAT)) & (row_lane < float(STAT + 32)), knn_lse, lse_row)
    stats = jnp.where(row_lane == float(COUNT), biggest, stats)
    send[ROWS] = meta + stats

    pl.semaphore_wait(barrier, n_dev - 1)

    def push(o, carry):
        to = lax.rem(me + o * 37, n_dev)
        pltpu.make_async_remote_copy(
            send.at[:, to], recv.at[:, me], send_sem, recv_sem, device_id={"model": to}, device_id_type=MESH
        ).start()
        return carry

    lax.fori_loop(1, n_dev, push, 0)
    recv[:, pl.ds(me, 1), :] = send[:, pl.ds(me, 1), :]
    others = recv.at[:, pl.ds(0, n_dev - 1)]
    pltpu.make_async_copy(others, others, recv_sem).wait()

    meta = recv[ROWS]
    peak = jnp.max(meta, axis=0, keepdims=True)
    grown = jnp.exp(meta - peak)
    sums = jnp.sum(grown, axis=0, keepdims=True)
    in_knn = (lane >= float(STAT)) & (lane < float(STAT + 32))
    share = jnp.where(in_knn, grown * (mix_ref[0] / sums), 0.0)
    share = share + pltpu.roll(share, 64, 1)
    share = share + pltpu.roll(share, 32, 1)
    lse = peak + jnp.log(sums)
    lse_col = jnp.sum(jnp.where(q_lane == q_sub + float(STAT + 32), lse, 0.0), axis=1, keepdims=True)
    plm_ref[...] = (1.0 - mix_ref[0]) * jnp.exp(logits - lse_col)
    cnt_ref[...] = jnp.broadcast_to(jnp.max(jnp.where(row_lane == float(COUNT), peak, 0.0), axis=1, keepdims=True), (1, LANES))

    for r in range(ROWS):
        parts = _split3(recv[r] * share)
        for k in range(3):
            x_ref[r * LANES : (r + 1) * LANES, k * LANES : (k + 1) * LANES] = parts[k]
    places = jnp.transpose(meta)
    vocab = _iota((2 * LANES, LANES), 0) + 1.0
    vgroup = jnp.floor(_iota((2 * LANES, LANES), 1) * (1.0 / 32.0))
    acc = jnp.zeros((2 * LANES, LANES), F32)
    for j in range(4):
        hot = jnp.concatenate(
            [jnp.where(vocab == places[4 * r + j : 4 * r + j + 1, :], 1.0, 0.0).astype(BF16) for r in range(ROWS)], axis=1
        )
        h = jnp.dot(hot, x_ref[...], preferred_element_type=F32)
        h = h[:, :LANES] + h[:, LANES : 2 * LANES] + h[:, 2 * LANES :]
        acc = jnp.where(vgroup == float(j), h, acc)
    flat = jnp.transpose(acc)
    p = flat[0:32] + flat[32:64] + flat[64:96] + flat[96:128]
    p_ref[...] = p[:, :v_loc]

    mine = send.at[:, pl.ds(0, n_dev - 1)]
    pltpu.make_async_copy(mine, mine, send_sem).wait()


def solution(mesh):
    n_dev = mesh.shape["model"]

    def local_step(queries, w_shard, key_shard, tok_shard, temperature, mix_weight):
        n_rows, dim = queries.shape
        n_keys, v_loc = key_shard.shape[0], w_shard.shape[1]
        tok = tok_shard.reshape(n_keys // LANES, LANES)
        any_space = pl.BlockSpec(memory_space=pl.ANY)
        smem = pl.BlockSpec(memory_space=pltpu.SMEM)
        vmem = pl.BlockSpec(memory_space=pltpu.VMEM)
        n_chunk = 8
        exchange = pl.pallas_call(
            functools.partial(_kernel, n_dev),
            out_shape=[
                jax.ShapeDtypeStruct((n_rows, v_loc), F32),
                jax.ShapeDtypeStruct((n_rows, v_loc), F32),
                jax.ShapeDtypeStruct((1, LANES), F32),
            ],
            in_specs=[smem, smem, smem, any_space, any_space, any_space, any_space],
            out_specs=[vmem, vmem, vmem],
            scratch_shapes=[
                pltpu.VMEM((n_rows, dim), BF16),
                pltpu.VMEM((dim, v_loc), BF16),
                pltpu.VMEM((n_keys, dim), BF16),
                pltpu.VMEM((n_keys // LANES, LANES), jnp.int32),
                pltpu.VMEM((n_dev, n_keys), BF16),
                pltpu.VMEM((ROWS * n_dev, n_keys), BF16),
                pltpu.VMEM((n_keys, 3 * LANES), BF16),
                pltpu.VMEM((n_keys, LANES), F32),
                pltpu.VMEM((n_keys, LANES), F32),
                pltpu.VMEM((ROWS + 1, n_dev, LANES), F32),
                pltpu.VMEM((ROWS + 1, n_dev, LANES), F32),
                pltpu.VMEM((ROWS * n_dev, 3 * LANES), BF16),
                pltpu.SemaphoreType.DMA((3,)),
                pltpu.SemaphoreType.DMA((n_chunk,)),
                pltpu.SemaphoreType.DMA,
                pltpu.SemaphoreType.DMA,
            ],
            compiler_params=pltpu.CompilerParams(
                collective_id=0, has_side_effects=True, vmem_limit_bytes=60 * 1024 * 1024
            ),
        )

        def run(r):
            return exchange(r.reshape(1), temperature, mix_weight, queries, w_shard, key_shard, tok)

        p_knn, p_lm, count = run(jnp.int32(0))
        rounds = lax.div(count[0, 0].astype(jnp.int32) + (CAP - 1), CAP)

        def more(state):
            return state[0] + 1, state[1] + run(state[0])[0]

        p_knn = lax.while_loop(lambda state: state[0] < rounds, more, (jnp.int32(1), p_knn))[1]
        return jnp.log(p_knn + p_lm)

    return jax.shard_map(
        local_step,
        mesh=mesh,
        in_specs=(P("data", None), P(None, "model"), P("model", None), P("model"), P(), P()),
        out_specs=P("data", "model"),
        check_vma=False,
    )
```

time: 280 us -> 40.7 us (0.15)
  blocking collectives: 131 us -> 0 us
  waiting for transfers between devices: 88.2 us -> 0 us
  Pallas kernels: 0 us -> 37 us
  other arithmetic: 25.9 us -> 0.63 us
  between operations: 14.7 us -> 2.13 us
  local copies, waits for them, and re-layouts: 11.7 us -> 0.57 us
  matrix products: 7.44 us -> 0 us
    unnamed x2 -> x0, waiting for transfers between devices: 88.2 us -> none
    pmax x1 -> x0, blocking collectives: 68.7 us -> none  [local_step(): row_max = lax.pmax(jnp.max(scores, axis=1), 'model')]
    psum x1 -> x0, blocking collectives: 62.8 us -> none  [local_step(): lm_total = lax.psum(jnp.sum(lm_exp, axis=1), 'model')]
    pallas_call x0 -> x1, Pallas kernels: none -> 37 us  [run(): exchange(r.reshape(1), temperature, mix_weight, queries, w_shard, key_sha...]
    scatter-add x1 -> x0, other arithmetic: 18.1 us -> none  [local_step(): jnp.zeros((row_count, vocab_size), jnp.float32).at[:, tok_shard]]
    scatter-add x1 -> x0, local copies, waits for them, and re-layouts: 11.4 us -> none  [local_step(): jnp.zeros((row_count, vocab_size), jnp.float32).at[:, tok_shard]]
    dot_general x2 -> x0, matrix products: 7.44 us -> none  [the longest x1 6.15 us: local_step(): jnp.einsum('bd,nd->bn', queries, key_shard, preferred_element_type=jnp.fl...]
    reduce_sum x3 -> x0, other arithmetic: 5.49 us -> none  [the longest x1 5.08 us: local_step(): key_sq = jnp.sum(jnp.square(key_shard.astype(jnp.float32)), axis=1)]
  transfers between devices with their start and end apart: 1 -> 0, of which waited for: 1 -> 0; matrix products, arithmetic and copies ran while one was open for 0% -> 0% of each run, Pallas kernels for 0% -> 0%
where the time goes in v1:
time: 40.7 us; the launch traced here: 40.5 us
  Pallas kernels  37 us (91%)
  between operations  2.13 us (5%)
  other arithmetic  0.63 us (2%)
  local copies, waits for them, and re-layouts  0.57 us (1%)
    pallas_call x1, Pallas kernels, run(): exchange(r.reshape(1), temperature, mix_weight, queries, w_shard, key_sha...  37 us

profile of v1, /device:TPU:1, one launch (start us, length us, event | category | flops | bytes accessed | tf_op | source)
XLA Modules:
  0.0 40.5 jit_solution(4178255762535157116)
XLA Ops:
  0.0 0.0 copy-start.2
  0.0 0.0 copy-start.1
  0.0 0.0 copy-start
  1.4 37.0 %shard_map.64 = (f32[32,250]{1,0:T(8,128)S(1)}, f32[32,250]{1,0:T(8,128)}, f32[1,128]{1,0:T(1,128)}) custom-call(s32[1]{0:T(128)} %constant.4.clone.1.rnd_ref, f32[1]{0:T(128)S(6)} %copy.13.tau_ref, f32[1]{0:T(128)S(6)} %copy.14.mix_ref, bf16[32,2048]{1,0:T(8,128)(2,1)} %q_hbm.1, bf16[2048,250]{1,0:T(8,128)(2,1)} %w_hbm.1, bf16[2048,2048]{1,0:T(8,128)(2,1)} %key_hbm.1, ...), custom_call_target="tpu_custom_call" | custom-call | tf_op jit(solution)/shard_map/pallas_call | solution.py:245
  39.1 0.0 copy-done.2
  39.1 0.0 copy-done.1
  39.1 0.0 copy-done
  39.1 0.0 copy-start.3
  39.1 0.2 while.10
  39.3 0.6 %copy-done.3 = f32[32,250]{1,0:T(8,128)S(1)} copy-done((f32[32,250]{1,0:T(8,128)S(1)}, f32[32,250]{1,0:T(8,128)}, u32[]{:S(2)}) %copy-start.3) | copy-done | bytes 32024
  39.9 0.6 %add_log_fusion = f32[32,250]{1,0:T(8,128)} fusion(f32[32,250]{1,0:T(8,128)S(1)} %get-tuple-element.59, f32[32,250]{1,0:T(8,128)S(1)} %copy-done.3), kind=kLoop, calls=%fused_computation | loop fusion | flops 8000 | bytes 96000 | tf_op jit(solution)/shard_map/log | solution.py:254
Async XLA Ops:
  0.0 39.1 %copy-start.2 = (s32[2048]{0:T(1024)S(1)}, s32[2048]{0:T(1024)}, u32[]{:S(2)}) copy-start(s32[2048]{0:T(1024)} %param.11) | copy-start | bytes 24580
  0.0 39.1 %copy-start.1 = (bf16[32,2048]{1,0:T(8,128)(2,1)S(1)}, bf16[32,2048]{1,0:T(8,128)(2,1)}, u32[]{:S(2)}) copy-start(bf16[32,2048]{1,0:T(8,128)(2,1)} %q_hbm.1) | copy-start | bytes 393220
  0.0 39.1 %copy-start = (bf16[2048,250]{1,0:T(8,128)(2,1)S(1)}, bf16[2048,250]{1,0:T(8,128)(2,1)}, u32[]{:S(2)}) copy-start(bf16[2048,250]{1,0:T(8,128)(2,1)} %w_hbm.1) | copy-start | bytes 3072004
  39.1 0.8 %copy-start.3 = (f32[32,250]{1,0:T(8,128)S(1)}, f32[32,250]{1,0:T(8,128)}, u32[]{:S(2)}) copy-start(f32[32,250]{1,0:T(8,128)} %get-tuple-element.60) | copy-start | bytes 96004

commit v2 on v0

v2 whole, which is shorter than its diff:
```python
import functools

import jax
import jax.numpy as jnp
from jax import lax
from jax.experimental import pallas as pl
from jax.experimental.pallas import tpu as pltpu
from jax.sharding import PartitionSpec as P

MESH = pl.DeviceIdType.MESH
F32 = jnp.float32
BF16 = jnp.bfloat16
LANES = 128
WIDE = 2 * LANES
DEPTH = 4
CAP = 8 * DEPTH
POOL = 4
ROWS = 2 * DEPTH + 1
PARTS = 2
HALF = 2
COUNT = 48
STAT = 64
EMPTY = 255.0


def _iota(shape, dim):
    return lax.broadcasted_iota(jnp.int32, shape, dim).astype(F32)


def _split3(x):
    hi = x.astype(BF16)
    rest = x - hi.astype(F32)
    mid = rest.astype(BF16)
    low = (rest - mid.astype(F32)).astype(BF16)
    return hi, mid, low


def _bucket(owner, source, n_dev):
    ahead = owner - source
    ahead = jnp.where(ahead < 0.0, ahead + float(n_dev), ahead)
    turn = jnp.floor(ahead * (1.0 / PARTS))
    return (ahead - PARTS * turn) * float(n_dev // PARTS) + turn


def _kernel(n_dev, whole, rnd_ref, tau_hbm, mix_hbm, q_hbm, w_hbm, key_hbm, tok_hbm, *refs):
    outs, refs = (refs[:2], refs[2:]) if whole else (refs[:3], refs[3:])
    (
        tau_ref, mix_ref, q_ref, w_ref, key_ref, tok_ref, hot_ref, pack_ref, place_ref, rhs_ref, s_ref, mask_ref,
        send, recv, x_ref, found_ref, in_sem, key_sem, send_sem, recv_sem,
    ) = refs
    me = lax.axis_index("model")
    me_f = me.astype(F32)
    n_rows, dim = q_ref.shape
    n_keys = key_ref.shape[0]
    v_loc = w_ref.shape[1]
    n_blk = n_keys // LANES
    n_chunk = key_sem.shape[0]
    step = n_keys // n_chunk
    group_len = n_dev // PARTS
    half_len = n_dev // HALF
    pool_at = DEPTH * group_len

    sources = [(tok_hbm, tok_ref), (q_hbm, q_ref), (w_hbm, w_ref), (tau_hbm, tau_ref), (mix_hbm, mix_ref)]
    loads = [pltpu.make_async_copy(src, dst, in_sem.at[i]) for i, (src, dst) in enumerate(sources)]
    key_loads = [
        pltpu.make_async_copy(key_hbm.at[pl.ds(i * step, step)], key_ref.at[pl.ds(i * step, step)], key_sem.at[i])
        for i in range(n_chunk)
    ]
    for load in loads + key_loads:
        load.start()

    barrier = pltpu.get_barrier_semaphore()
    for o in range(1, n_dev):
        pl.semaphore_signal(barrier, inc=1, device_id={"model": lax.rem(me + o, n_dev)}, device_id_type=MESH)

    loads[0].wait()
    tok = tok_ref[...].astype(F32)
    owner = jnp.floor((tok + 0.5) * (1.0 / v_loc))
    place = tok - owner * v_loc + 1.0
    bucket = _bucket(owner, me_f, n_dev)
    sub = _iota((LANES, LANES), 0)
    lane = _iota((LANES, LANES), 1)
    diag = sub == lane
    ones = jnp.ones((LANES, LANES), BF16)
    upper = jnp.where(sub <= lane, 1.0, 0.0).astype(BF16)
    tri = jnp.concatenate([upper, ones], axis=1)
    for c in range(n_blk):
        hot_ref[:, c * LANES : (c + 1) * LANES] = jnp.where(sub == bucket[c : c + 1, :], 1.0, 0.0).astype(BF16)
    ranks = []
    for c in range(0, n_blk, 4):
        hot_rows = jnp.concatenate([hot_ref[:, k * LANES : (k + 1) * LANES] for k in range(c, c + 4)], axis=0)
        part = jnp.dot(hot_rows, tri, preferred_element_type=F32)
        ranks += [part[k * LANES : (k + 1) * LANES] for k in range(4)]
    before = jnp.zeros((LANES, LANES), F32)
    first = 1.0 if whole else rnd_ref[0].astype(F32) * float(CAP) + 1.0
    slots = []
    for c in range(n_blk):
        mine = sub == bucket[c : c + 1, :]
        slots.append(jnp.sum(jnp.where(mine, ranks[c][:, :LANES] + before, 0.0), axis=0, keepdims=True) - first)
        before = before + ranks[c][:, LANES:]
    slot = jnp.concatenate(slots, axis=0)
    if whole:
        over = jnp.where(slot >= float(CAP), 1.0, 0.0)
        inside = jnp.dot(over.astype(BF16), tri, preferred_element_type=F32)
        lower = jnp.where(_iota((n_blk, n_blk), 0) > _iota((n_blk, n_blk), 1), 1.0, 0.0).astype(BF16)
        ahead = jnp.dot(lower, inside[:, LANES:].astype(BF16), preferred_element_type=F32)
        rank = ahead + inside[:, :LANES] - 1.0
        code = jnp.where(rank < float(POOL), rank + float(CAP), EMPTY)
        code = jnp.where(slot < float(CAP), slot, code)
        demand = (ahead + inside[:, LANES:])[n_blk - 1 : n_blk]
    else:
        code = jnp.where((slot >= 0.0) & (slot < float(CAP)), slot, EMPTY)
        demand = jnp.max(before, axis=0, keepdims=True)
    depth = jnp.floor(code * 0.125)
    lane_group = jnp.floor(lane * (1.0 / 32.0))

    def sort_block(c):
        rows = pl.ds(c * LANES, LANES)
        cols = slice(c * LANES, (c + 1) * LANES)
        both = jnp.concatenate(
            [jnp.where(diag, code[c : c + 1, :], 0.0), jnp.where(diag, place[c : c + 1, :], 0.0)], axis=0
        )
        both = jnp.dot(both.astype(BF16), ones, preferred_element_type=F32)
        code_col, place_col = both[:LANES], both[LANES:]
        place_ref[rows, :] = jnp.where(code_col == lane, place_col, 0.0).astype(BF16)
        eighth = code_col - 8.0 * jnp.floor(code_col * 0.125)
        mask_ref[rows, :LANES] = jnp.where(eighth == lane_group, 1.0, 0.0).astype(BF16)
        mask_ref[rows, LANES:] = jnp.where(eighth == lane_group + 4.0, 1.0, 0.0).astype(BF16)
        hot = hot_ref[:, cols]
        for r in range(DEPTH):
            keep = jnp.broadcast_to(jnp.where(depth[c : c + 1, :] == float(r), 1.0, 0.0), (LANES, LANES)).astype(BF16)
            kept = hot * keep
            for g in range(PARTS):
                at = g * (pool_at + 16) + r * group_len
                pack_ref[at : at + group_len, cols] = kept[g * group_len : (g + 1) * group_len]
        spare = jnp.where((depth[c : c + 1, :] == float(DEPTH)) & (_iota((16, LANES), 0) == 0.0), 1.0, 0.0)
        pack_ref[pool_at : pool_at + 16, cols] = spare.astype(BF16)

    for load in loads[1:]:
        load.wait()
    q = q_ref[...]
    logits = jnp.dot(q, w_ref[...], preferred_element_type=F32)
    lm_max = jnp.max(logits, axis=1, keepdims=True)
    lm_lse = lm_max + jnp.log(jnp.sum(jnp.exp(logits - lm_max), axis=1, keepdims=True))
    q_sub = _iota((n_rows, LANES), 0)
    q_lane = _iota((n_rows, LANES), 1)
    knn_diag = q_lane == q_sub + float(STAT)
    lm_diag = q_lane == q_sub + float(STAT + 32)
    lse_row = jnp.sum(jnp.where(lm_diag, lm_lse, 0.0), axis=0, keepdims=True)

    q4 = jnp.concatenate([q, q, q, q], axis=0)
    inv_tau = 1.0 / jnp.full((1, LANES), tau_ref[0], F32)
    tops, totals = [], []
    fine = step // 2
    for i in range(n_chunk):
        key_loads[i].wait()
        for c in range(i * n_blk // n_chunk, (i + 1) * n_blk // n_chunk):
            sort_block(c)
        for j in range(2):
            rows = pl.ds(i * step + j * fine, fine)
            dots = lax.dot_general(key_ref[rows, :], q4, (((1,), (1,)), ((), ())), preferred_element_type=F32)
            sq = jnp.zeros((fine, LANES), F32)
            for t in range(dim // LANES):
                k = key_ref[rows, t * LANES : (t + 1) * LANES].astype(F32)
                sq = sq + k * k
            s = (2.0 * dots - jnp.sum(sq, axis=1, keepdims=True)) * inv_tau
            top = jnp.max(s, axis=0, keepdims=True)
            e = jnp.exp(s - top)
            s_ref[rows, :] = e
            tops.append(top)
            totals.append(jnp.sum(e, axis=0, keepdims=True))
    top = functools.reduce(jnp.maximum, tops)
    shrink = [jnp.exp(t - top) for t in tops]
    total = sum(a * b for a, b in zip(shrink, totals))
    scale = 1.0 / total
    knn_lse = top + jnp.log(total)
    for i in range(2 * n_chunk):
        rows = pl.ds(i * fine, fine)
        parts = _split3(s_ref[rows, :] * (shrink[i] * scale))
        for k in range(3):
            for b in range(2):
                at = k * WIDE + b * LANES
                rhs_ref[rows, at : at + LANES] = parts[k] * mask_ref[rows, b * LANES : (b + 1) * LANES]

    row_lane = _iota((1, LANES), 1)
    in_knn = (row_lane >= float(STAT)) & (row_lane < float(STAT + 32))
    stats = jnp.where(in_knn, knn_lse, lse_row)
    stats = jnp.where(row_lane == float(COUNT), demand, stats)
    places = jnp.dot(hot_ref[...], place_ref[...], preferred_element_type=F32)
    in_pool = (row_lane >= float(CAP)) & (row_lane < float(CAP + POOL))
    pool_place = jnp.where(in_pool, jnp.sum(places, axis=0, keepdims=True), 0.0)
    pool_bucket = jnp.sum(jnp.where(places > 0.0, sub + 1.0, 0.0), axis=0, keepdims=True)
    pool_bucket = jnp.where(in_pool, pool_bucket, 0.0)
    pool_bucket = pltpu.roll(jnp.broadcast_to(pool_bucket, (8, LANES)), POOL, 1)[:1]
    send[ROWS] = jnp.where(lane < float(CAP), places, 0.0) + (stats + pool_place + pool_bucket)
    for g in range(PARTS):
        base = g * (pool_at + 16)
        span = pool_at + (16 if g == 0 else 0)
        packed = jnp.dot(pack_ref[base : base + span, :], rhs_ref[...], preferred_element_type=F32)
        packed = packed[:, :WIDE] + packed[:, WIDE : 2 * WIDE] + packed[:, 2 * WIDE :]
        for r in range(DEPTH):
            for b in range(2):
                send[2 * r + b, g * group_len : (g + 1) * group_len] = packed[
                    r * group_len : (r + 1) * group_len, b * LANES : (b + 1) * LANES
                ]
        if g == 0:
            send[2 * DEPTH] = jnp.broadcast_to(packed[pool_at : pool_at + 1, :LANES], (n_dev, LANES))
            pl.semaphore_wait(barrier, n_dev - 1)
        for o in range(group_len):
            turn = (o * 29 + 29) % group_len
            if PARTS * turn + g == 0:
                continue
            pltpu.make_async_remote_copy(
                send.at[:, g * group_len + turn], recv.at[:, me], send_sem, recv_sem.at[me // half_len],
                device_id={"model": lax.rem(me + (PARTS * turn + g), n_dev)}, device_id_type=MESH,
            ).start()
    recv[:, pl.ds(me, 1), :] = send[:, 0:1, :]

    vocab = (_iota((WIDE, LANES), 0) + 1.0).astype(BF16)
    n_pair = (ROWS + 1) // 2
    peaks, sums, hists = [], [], []
    for h in range(HALF):
        inside = me // half_len == h

        @pl.when(inside)
        def _():
            landed = recv.at[:, pl.ds(0, half_len - 1)]
            pltpu.make_async_copy(landed, landed, recv_sem.at[h]).wait()

        @pl.when(jnp.logical_not(inside))
        def _():
            landed = recv.at[:, pl.ds(0, half_len)]
            pltpu.make_async_copy(landed, landed, recv_sem.at[h]).wait()

        span = slice(h * half_len, (h + 1) * half_len)
        meta = recv[ROWS, span]
        peak = jnp.max(meta, axis=0, keepdims=True)
        grown = jnp.exp(meta - peak)
        peaks.append(peak)
        sums.append(jnp.sum(grown, axis=0, keepdims=True))
        share = jnp.where(in_knn, grown, 0.0)
        share = share + pltpu.roll(share, 64, 1)
        share = share + pltpu.roll(share, 32, 1)
        by_lane = jnp.transpose(jnp.concatenate([meta, meta], axis=0))
        from_lane = lax.rem(lax.broadcasted_iota(jnp.int32, (1, LANES), 1), half_len) + h * half_len
        my_bucket = _bucket(me_f, from_lane.astype(F32), n_dev) + 1.0
        first_half = row_lane < float(half_len)
        for pair in range(n_pair):
            a, b = 2 * pair, 2 * pair + 1
            xa = recv[a, span] * share
            xb = recv[b, span] * share if b < ROWS else jnp.zeros_like(xa)
            parts = _split3(jnp.transpose(jnp.concatenate([xa, xb], axis=0)))
            for j in range(4):
                at = (j * n_pair + pair) * LANES
                for k in range(3):
                    x_ref[h, k * n_rows : (k + 1) * n_rows, at : at + LANES] = parts[k][j * n_rows : (j + 1) * n_rows]
                place_a = by_lane[4 * a + j : 4 * a + j + 1]
                if b < ROWS:
                    place_b = by_lane[4 * b + j : 4 * b + j + 1]
                else:
                    place_a = jnp.where(by_lane[CAP + POOL + j : CAP + POOL + j + 1] == my_bucket, place_a, 0.0)
                    place_b = jnp.zeros_like(place_a)
                wanted = jnp.broadcast_to(jnp.where(first_half, place_a, place_b), (WIDE, LANES)).astype(BF16)
                found_ref[h, :, at : at + LANES] = jnp.where(vocab == wanted, jnp.ones((), BF16), jnp.zeros((), BF16))
        hist = jnp.zeros((n_rows, WIDE), F32)
        cut = 2 * n_pair * LANES
        for j in range(2):
            got = lax.dot_general(
                x_ref[h, :, j * cut : (j + 1) * cut], found_ref[h, :, j * cut : (j + 1) * cut],
                (((1,), (1,)), ((), ())), preferred_element_type=F32,
            )
            hist = hist + (got[:n_rows] + got[n_rows : 2 * n_rows] + got[2 * n_rows :])
        hists.append(hist)
    peak = functools.reduce(jnp.maximum, peaks)
    shrink = [jnp.exp(p - peak) for p in peaks]
    total = sum(a * b for a, b in zip(shrink, sums))
    lse = peak + jnp.log(total)
    lse_col = jnp.sum(jnp.where(lm_diag, lse, 0.0), axis=1, keepdims=True)
    p_lm = (1.0 - mix_ref[0]) * jnp.exp(logits - lse_col)
    share = mix_ref[0] / total
    p_knn = sum(
        a * jnp.sum(jnp.where(knn_diag, s * share, 0.0), axis=1, keepdims=True) for a, s in zip(hists, shrink)
    )[:, :v_loc]
    if whole:
        outs[0][...] = jnp.log(p_knn + p_lm)
    else:
        outs[0][...] = p_knn
        outs[1][...] = p_lm
    most = jnp.max(jnp.where(row_lane == float(COUNT), peak, 0.0), axis=1, keepdims=True)
    outs[-1][...] = jnp.broadcast_to(most, (1, LANES))

    mine = send.at[:, pl.ds(0, n_dev - 1)]
    pltpu.make_async_copy(mine, mine, send_sem).wait()


def solution(mesh):
    n_dev = mesh.shape["model"]

    def local_step(queries, w_shard, key_shard, tok_shard, temperature, mix_weight):
        n_rows, dim = queries.shape
        n_keys, v_loc = key_shard.shape[0], w_shard.shape[1]
        tok = tok_shard.reshape(n_keys // LANES, LANES)
        any_space = pl.BlockSpec(memory_space=pl.ANY)
        smem = pl.BlockSpec(memory_space=pltpu.SMEM)
        vmem = pl.BlockSpec(memory_space=pltpu.VMEM)
        n_chunk = 4
        n_pair = (ROWS + 1) // 2

        def exchange(whole, r):
            block = jax.ShapeDtypeStruct((n_rows, v_loc), F32)
            shapes = [block] if whole else [block, block]
            return pl.pallas_call(
                functools.partial(_kernel, n_dev, whole),
                out_shape=shapes + [jax.ShapeDtypeStruct((1, LANES), F32)],
                in_specs=[smem] + [any_space] * 6,
                out_specs=[vmem] * (len(shapes) + 1),
                scratch_shapes=[
                    pltpu.SMEM((1,), F32),
                    pltpu.SMEM((1,), F32),
                    pltpu.VMEM((n_rows, dim), BF16),
                    pltpu.VMEM((dim, v_loc), BF16),
                    pltpu.VMEM((n_keys, dim), BF16),
                    pltpu.VMEM((n_keys // LANES, LANES), jnp.int32),
                    pltpu.VMEM((n_dev, n_keys), BF16),
                    pltpu.VMEM((DEPTH * n_dev + 16, n_keys), BF16),
                    pltpu.VMEM((n_keys, LANES), BF16),
                    pltpu.VMEM((n_keys, 3 * WIDE), BF16),
                    pltpu.VMEM((n_keys, LANES), F32),
                    pltpu.VMEM((n_keys, WIDE), BF16),
                    pltpu.VMEM((ROWS + 1, n_dev, LANES), F32),
                    pltpu.VMEM((ROWS + 1, n_dev, LANES), F32),
                    pltpu.VMEM((HALF, 3 * n_rows, 4 * n_pair * LANES), BF16),
                    pltpu.VMEM((HALF, WIDE, 4 * n_pair * LANES), BF16),
                    pltpu.SemaphoreType.DMA((5,)),
                    pltpu.SemaphoreType.DMA((n_chunk,)),
                    pltpu.SemaphoreType.DMA,
                    pltpu.SemaphoreType.DMA((HALF,)),
                ],
                compiler_params=pltpu.CompilerParams(
                    collective_id=0 if whole else 1, has_side_effects=True, vmem_limit_bytes=60 * 1024 * 1024
                ),
            )(r.reshape(1), temperature, mix_weight, queries, w_shard, key_shard, tok)

        out, demand = exchange(True, jnp.int32(0))

        def in_rounds(unused):
            zero = jnp.zeros((n_rows, v_loc), F32)

            def step(carry):
                r, unused, p_knn, unused_lm = carry
                more, p_lm, biggest = exchange(False, r)
                return r + 1, biggest[0, 0], p_knn + more, p_lm

            state = (jnp.int32(0), jnp.float32(1), zero, zero)
            state = lax.while_loop(lambda carry: (carry[0] * CAP).astype(F32) < carry[1], step, state)
            return jnp.log(state[2] + state[3])

        return lax.cond(demand[0, 0] > float(POOL), in_rounds, lambda done: done, out)

    return jax.shard_map(
        local_step,
        mesh=mesh,
        in_specs=(P("data", None), P(None, "model"), P("model", None), P("model"), P(), P()),
        out_specs=P("data", "model"),
        check_vma=False,
    )
```

time: 280 us -> 32.2 us (0.12)
  blocking collectives: 131 us -> 0 us
  waiting for transfers between devices: 88.2 us -> 0 us
  Pallas kernels: 0 us -> 29.3 us
  other arithmetic: 25.9 us -> 0 us
  between operations: 14.7 us -> 2 us
  local copies, waits for them, and re-layouts: 11.7 us -> 0.63 us
  matrix products: 7.44 us -> 0 us
    unnamed x2 -> x0, waiting for transfers between devices: 88.2 us -> none
    pmax x1 -> x0, blocking collectives: 68.7 us -> none  [local_step(): row_max = lax.pmax(jnp.max(scores, axis=1), 'model')]
    psum x1 -> x0, blocking collectives: 62.8 us -> none  [local_step(): lm_total = lax.psum(jnp.sum(lm_exp, axis=1), 'model')]
    pallas_call x0 -> x1, Pallas kernels: none -> 29.3 us  [exchange(): pl.pallas_call(functools.partial(_kernel, n_dev, whole), out_shape=shapes...]
    scatter-add x1 -> x0, other arithmetic: 18.1 us -> none  [local_step(): jnp.zeros((row_count, vocab_size), jnp.float32).at[:, tok_shard]]
    scatter-add x1 -> x0, local copies, waits for them, and re-layouts: 11.4 us -> none  [local_step(): jnp.zeros((row_count, vocab_size), jnp.float32).at[:, tok_shard]]
    dot_general x2 -> x0, matrix products: 7.44 us -> none  [the longest x1 6.15 us: local_step(): jnp.einsum('bd,nd->bn', queries, key_shard, preferred_element_type=jnp.fl...]
    reduce_sum x3 -> x0, other arithmetic: 5.49 us -> none  [the longest x1 5.08 us: local_step(): key_sq = jnp.sum(jnp.square(key_shard.astype(jnp.float32)), axis=1)]
  transfers between devices with their start and end apart: 1 -> 0, of which waited for: 1 -> 0; matrix products, arithmetic and copies ran while one was open for 0% -> 0% of each run, Pallas kernels for 0% -> 0%
where the time goes in v2:
time: 32.2 us; the launch traced here: 32.1 us
  Pallas kernels  29.3 us (91%)
  between operations  2 us (6%)
  local copies, waits for them, and re-layouts  0.63 us (2%)
    pallas_call x1, Pallas kernels, exchange(): pl.pallas_call(functools.partial(_kernel, n_dev, whole), out_shape=shapes...  29.3 us

profile of v2, /device:TPU:1, one launch (start us, length us, event | category | flops | bytes accessed | tf_op | source)
XLA Modules:
  0.0 32.1 jit_solution(10965368121804783025)
XLA Ops:
  0.0 0.0 copy-start
  0.0 0.0 copy-start.1
  0.0 0.0 copy-start.2
  1.4 29.3 %shard_map.66 = (f32[32,250]{1,0:T(8,128)S(1)}, f32[1,128]{1,0:T(1,128)}) custom-call(s32[1]{0:T(128)} %constant.7.clone.1.rnd_ref, f32[1]{0:T(128)S(6)} %copy.26.tau_hbm, f32[1]{0:T(128)S(6)} %copy.27.mix_hbm, bf16[32,2048]{1,0:T(8,128)(2,1)} %q_hbm.1, bf16[2048,250]{1,0:T(8,128)(2,1)} %w_hbm.1, bf16[2048,2048]{1,0:T(8,128)(2,1)} %key_hbm.1, s32[16,128]{1,0:T(8,128)} %bitcast.12), custom_call_target="tpu_custom_call" | custom-call | tf_op jit(solution)/shard_map/pallas_call | solution.py:312
  31.3 0.0 copy-done
  31.3 0.0 copy-done.1
  31.3 0.0 copy-done.2
  31.3 0.2 conditional.1
  31.5 0.6 %copy.30 = f32[32,250]{1,0:T(8,128)} copy(f32[32,250]{1,0:T(8,128)S(1)} %get-tuple-element.86) | data formatting | bytes 64000
Async XLA Ops:
  0.0 31.3 %copy-start = (bf16[2048,250]{1,0:T(8,128)(2,1)S(1)}, bf16[2048,250]{1,0:T(8,128)(2,1)}, u32[]{:S(2)}) copy-start(bf16[2048,250]{1,0:T(8,128)(2,1)} %w_hbm.1) | copy-start | bytes 3072004
  0.0 31.3 %copy-start.1 = (bf16[32,2048]{1,0:T(8,128)(2,1)S(1)}, bf16[32,2048]{1,0:T(8,128)(2,1)}, u32[]{:S(2)}) copy-start(bf16[32,2048]{1,0:T(8,128)(2,1)} %q_hbm.1) | copy-start | bytes 393220
  0.0 31.3 %copy-start.2 = (s32[2048]{0:T(1024)S(1)}, s32[2048]{0:T(1024)}, u32[]{:S(2)}) copy-start(s32[2048]{0:T(1024)} %param.13) | copy-start | bytes 24580

commit v3 on v2

v3 whole, which is shorter than its diff:
```python
import functools

import jax
import jax.numpy as jnp
from jax import lax
from jax.experimental import pallas as pl
from jax.experimental.pallas import tpu as pltpu
from jax.sharding import PartitionSpec as P

MESH = pl.DeviceIdType.MESH
F32 = jnp.float32
BF16 = jnp.bfloat16
LANES = 128
WIDE = 2 * LANES
DEPTH = 4
CAP = 8 * DEPTH
POOL = 4
ROWS = 2 * DEPTH + 1
PARTS = 2
HALF = 2
COUNT = 48
STAT = 64
EMPTY = 255.0
CHUNKS = (512, 512, 512, 512)
SORTED = (8, 12, 16, 16)
FINE = 256


def _iota(shape, dim):
    return lax.broadcasted_iota(jnp.int32, shape, dim).astype(F32)


def _split3(x):
    hi = x.astype(BF16)
    rest = x - hi.astype(F32)
    mid = rest.astype(BF16)
    low = (rest - mid.astype(F32)).astype(BF16)
    return hi, mid, low


def _bucket(turn, n_dev):
    return lax.rem(turn, PARTS) * (n_dev // PARTS) + lax.div(turn, PARTS)


def _kernel(n_dev, whole, rnd_ref, tau_hbm, mix_hbm, q_hbm, w_hbm, key_hbm, tok_hbm, *refs):
    outs, refs = (refs[:2], refs[2:]) if whole else (refs[:3], refs[3:])
    (
        tau_ref, mix_ref, q_ref, w_ref, key_ref, tok_ref, hot_ref, pack_ref, place_ref, rhs_ref, s_ref, mask_ref,
        fac_ref, send, recv, x_ref, found_ref, in_sem, key_sem, send_sem, recv_sem,
    ) = refs
    me = lax.axis_index("model")
    n_rows, dim = q_ref.shape
    n_keys = key_ref.shape[1]
    v_loc = w_ref.shape[1]
    n_blk = n_keys // LANES
    n_tile = dim // LANES
    starts = [sum(CHUNKS[:i]) for i in range(len(CHUNKS))]
    group_len = n_dev // PARTS
    half_len = n_dev // HALF
    pool_at = DEPTH * group_len

    sources = [(tok_hbm, tok_ref), (q_hbm, q_ref), (w_hbm, w_ref), (tau_hbm, tau_ref), (mix_hbm, mix_ref)]
    loads = [pltpu.make_async_copy(src, dst, in_sem.at[i]) for i, (src, dst) in enumerate(sources)]
    for load in loads:
        load.start()
    for i, (at, size) in enumerate(zip(starts, CHUNKS)):
        for t in range(n_tile):
            pltpu.make_async_copy(
                key_hbm.at[pl.ds(at, size), pl.ds(t * LANES, LANES)], key_ref.at[t, pl.ds(at, size)], key_sem.at[i]
            ).start()

    barrier = pltpu.get_barrier_semaphore()
    for o in range(1, n_dev):
        pl.semaphore_signal(barrier, inc=1, device_id={"model": jnp.bitwise_xor(me, o)}, device_id_type=MESH)

    loads[0].wait()
    tok = tok_ref[...].astype(F32)
    owner = jnp.floor((tok + 0.5) * (1.0 / v_loc))
    place = tok - owner * v_loc + 1.0
    bucket = _bucket(jnp.bitwise_xor(owner.astype(jnp.int32), me), n_dev).astype(F32)
    sub = _iota((LANES, LANES), 0)
    lane = _iota((LANES, LANES), 1)
    ones = jnp.ones((LANES, LANES), BF16)
    upper = jnp.where(sub <= lane, 1.0, 0.0).astype(BF16)
    tri = jnp.concatenate([upper, ones], axis=1)
    for c in range(n_blk):
        hot_ref[c] = jnp.where(sub == bucket[c : c + 1, :], 1.0, 0.0).astype(BF16)
    ranks = []
    for c in range(0, n_blk, 4):
        hot_rows = jnp.concatenate([hot_ref[k] for k in range(c, c + 4)], axis=0)
        part = jnp.dot(hot_rows, tri, preferred_element_type=F32)
        ranks += [part[k * LANES : (k + 1) * LANES] for k in range(4)]
    before = jnp.zeros((LANES, LANES), F32)
    first = 1.0 if whole else rnd_ref[0].astype(F32) * float(CAP) + 1.0
    slots = []
    for c in range(n_blk):
        mine = sub == bucket[c : c + 1, :]
        slots.append(jnp.sum(jnp.where(mine, ranks[c][:, :LANES] + before, 0.0), axis=0, keepdims=True) - first)
        before = before + ranks[c][:, LANES:]
    slot = jnp.concatenate(slots, axis=0)
    if whole:
        over = jnp.where(slot >= float(CAP), 1.0, 0.0)
        inside = jnp.dot(over.astype(BF16), tri, preferred_element_type=F32)
        lower = jnp.where(_iota((n_blk, n_blk), 0) > _iota((n_blk, n_blk), 1), 1.0, 0.0).astype(BF16)
        ahead = jnp.dot(lower, inside[:, LANES:].astype(BF16), preferred_element_type=F32)
        rank = ahead + inside[:, :LANES] - 1.0
        code = jnp.where(rank < float(POOL), rank + float(CAP), EMPTY)
        code = jnp.where(slot < float(CAP), slot, code)
        demand = (ahead + inside[:, LANES:])[n_blk - 1 : n_blk]
    else:
        code = jnp.where((slot >= 0.0) & (slot < float(CAP)), slot, EMPTY)
        demand = jnp.max(before, axis=0, keepdims=True)
    depth = jnp.floor(code * 0.125)
    lane_group = jnp.floor(lane * (1.0 / 32.0))

    columns = jnp.transpose(jnp.concatenate([code, place] + [code] * (LANES // n_blk - 2), axis=0))

    def sort_block(c):
        rows = pl.ds(c * LANES, LANES)
        code_col = jnp.broadcast_to(columns[:, c : c + 1], (LANES, LANES))
        place_col = jnp.broadcast_to(columns[:, n_blk + c : n_blk + c + 1], (LANES, LANES))
        place_ref[rows, :] = jnp.where(code_col == lane, place_col, 0.0).astype(BF16)
        eighth = code_col - 8.0 * jnp.floor(code_col * 0.125)
        mask_ref[0, rows, :] = jnp.where(eighth == lane_group, 1.0, 0.0).astype(BF16)
        mask_ref[1, rows, :] = jnp.where(eighth == lane_group + 4.0, 1.0, 0.0).astype(BF16)
        hot = hot_ref[c]
        for r in range(DEPTH):
            keep = jnp.broadcast_to(jnp.where(depth[c : c + 1, :] == float(r), 1.0, 0.0), (LANES, LANES)).astype(BF16)
            kept = hot * keep
            for g in range(PARTS):
                at = g * (pool_at + 16) + r * group_len
                pack_ref[c, at : at + group_len] = kept[g * group_len : (g + 1) * group_len]
        spare = jnp.where((depth[c : c + 1, :] == float(DEPTH)) & (_iota((16, LANES), 0) == 0.0), 1.0, 0.0)
        pack_ref[c, pool_at : pool_at + 16] = spare.astype(BF16)

    for load in loads[1:]:
        load.wait()
    q = q_ref[...]
    logits = jnp.dot(q, w_ref[...], preferred_element_type=F32)
    lm_max = jnp.max(logits, axis=1, keepdims=True)
    lm_lse = lm_max + jnp.log(jnp.sum(jnp.exp(logits - lm_max), axis=1, keepdims=True))
    q_sub = _iota((n_rows, LANES), 0)
    q_lane = _iota((n_rows, LANES), 1)
    knn_diag = q_lane == q_sub + float(STAT)
    lm_diag = q_lane == q_sub + float(STAT + 32)
    lse_row = jnp.sum(jnp.where(lm_diag, lm_lse, 0.0), axis=0, keepdims=True)

    q4 = jnp.concatenate([q, q, q, q], axis=0)
    inv_tau = 1.0 / jnp.broadcast_to(tau_ref[...], (1, LANES))
    tops, totals = [], []

    def dots(i):
        for j in range(2):
            rows = pl.ds(starts[i] + j * CHUNKS[i] // 2, CHUNKS[i] // 2)
            keys = jnp.concatenate([key_ref[t, rows, :] for t in range(n_tile)], axis=1)
            s_ref[rows, :] = lax.dot_general(keys, q4, (((1,), (1,)), ((), ())), preferred_element_type=F32)

    def weigh(i):
        for j in range(CHUNKS[i] // FINE):
            rows = pl.ds(starts[i] + j * FINE, FINE)
            sq = jnp.zeros((FINE, LANES), F32)
            for t in range(n_tile):
                k = key_ref[t, rows, :].astype(F32)
                sq = sq + k * k
            s = (2.0 * s_ref[rows, :] - jnp.sum(sq, axis=1, keepdims=True)) * inv_tau
            top = jnp.max(s, axis=0, keepdims=True)
            e = jnp.exp(s - top)
            s_ref[rows, :] = e
            tops.append(top)
            totals.append(jnp.sum(e, axis=0, keepdims=True))

    sorted_up_to = 0
    for i in range(len(CHUNKS)):
        landed = key_ref.at[:, pl.ds(starts[i], CHUNKS[i])]
        pltpu.make_async_copy(landed, landed, key_sem.at[i]).wait()
        dots(i)
        for c in range(sorted_up_to, SORTED[i]):
            sort_block(c)
        sorted_up_to = SORTED[i]
        if i:
            weigh(i - 1)
    weigh(len(CHUNKS) - 1)
    top = functools.reduce(jnp.maximum, tops)
    shrink = [jnp.exp(t - top) for t in tops]
    total = sum(a * b for a, b in zip(shrink, totals))
    scale = 1.0 / total
    knn_lse = top + jnp.log(total)
    for i in range(n_keys // FINE):
        fac_ref[i] = jnp.broadcast_to(shrink[i] * scale, (8, LANES))

    def divide(i, carry):
        rows = pl.ds(pl.multiple_of(i * FINE, FINE), FINE)
        parts = _split3(s_ref[rows, :] * fac_ref[i][:1])
        for k in range(3):
            for m in range(2):
                rhs_ref[2 * k + m, rows, :] = parts[k] * mask_ref[m, rows, :]
        return carry

    lax.fori_loop(0, n_keys // FINE, divide, 0)

    row_lane = _iota((1, LANES), 1)
    in_knn = (row_lane >= float(STAT)) & (row_lane < float(STAT + 32))
    stats = jnp.where(in_knn, knn_lse, lse_row)
    stats = jnp.where(row_lane == float(COUNT), demand, stats)
    hot = jnp.concatenate([hot_ref[c] for c in range(n_blk)], axis=1)
    places = jnp.dot(hot, place_ref[...], preferred_element_type=F32)
    in_pool = (row_lane >= float(CAP)) & (row_lane < float(CAP + POOL))
    pool_place = jnp.where(in_pool, jnp.sum(places, axis=0, keepdims=True), 0.0)
    pool_bucket = jnp.sum(jnp.where(places > 0.0, sub + 1.0, 0.0), axis=0, keepdims=True)
    pool_bucket = jnp.where(in_pool, pool_bucket, 0.0)
    pool_bucket = pltpu.roll(jnp.broadcast_to(pool_bucket, (8, LANES)), POOL, 1)[:1]
    send[ROWS] = jnp.where(lane < float(CAP), places, 0.0) + (stats + pool_place + pool_bucket)
    for g in range(PARTS):
        base = g * (pool_at + 16)
        span = pool_at + (16 if g == 0 else 0)
        packed = []
        for lo, hi in ((0, pool_at // 2), (pool_at // 2, span)):
            lhs = jnp.concatenate([pack_ref[c, base + lo : base + hi, :] for c in range(n_blk)], axis=1)
            rhs = jnp.concatenate([rhs_ref[k] for k in range(6)], axis=1)
            got = jnp.dot(lhs, rhs, preferred_element_type=F32)
            packed.append(got[:, :WIDE] + got[:, WIDE : 2 * WIDE] + got[:, 2 * WIDE :])
        packed = jnp.concatenate(packed, axis=0)
        for r in range(DEPTH):
            for b in range(2):
                send[2 * r + b, g * group_len : (g + 1) * group_len] = packed[
                    r * group_len : (r + 1) * group_len, b * LANES : (b + 1) * LANES
                ]
        if g == 0:
            send[2 * DEPTH] = jnp.broadcast_to(packed[pool_at : pool_at + 1, :LANES], (n_dev, LANES))
            pl.semaphore_wait(barrier, n_dev - 1)
        for o in range(group_len):
            at = (o * 29 + 29) % group_len
            turn = PARTS * at + g
            if turn == 0:
                continue
            pltpu.make_async_remote_copy(
                send.at[:, g * group_len + at], recv.at[:, me], send_sem, recv_sem.at[me // half_len],
                device_id={"model": jnp.bitwise_xor(me, turn)}, device_id_type=MESH,
            ).start()
    recv[:, pl.ds(me, 1), :] = send[:, 0:1, :]

    vocab = (_iota((WIDE, LANES), 0) + 1.0).astype(BF16)
    n_pair = (ROWS + 1) // 2
    peaks, sums, hists = [], [], []
    for h in range(HALF):
        inside = me // half_len == h

        @pl.when(inside)
        def _():
            landed = recv.at[:, pl.ds(0, half_len - 1)]
            pltpu.make_async_copy(landed, landed, recv_sem.at[h]).wait()

        @pl.when(jnp.logical_not(inside))
        def _():
            landed = recv.at[:, pl.ds(0, half_len)]
            pltpu.make_async_copy(landed, landed, recv_sem.at[h]).wait()

        span = slice(h * half_len, (h + 1) * half_len)
        meta = recv[ROWS, span]
        peak = jnp.max(meta, axis=0, keepdims=True)
        grown = jnp.exp(meta - peak)
        peaks.append(peak)
        sums.append(jnp.sum(grown, axis=0, keepdims=True))
        share = jnp.where(in_knn, grown, 0.0)
        share = share + pltpu.roll(share, 64, 1)
        share = share + pltpu.roll(share, 32, 1)
        by_lane = jnp.transpose(jnp.concatenate([meta, meta], axis=0))
        from_lane = lax.rem(lax.broadcasted_iota(jnp.int32, (1, LANES), 1), half_len) + h * half_len
        my_bucket = _bucket(jnp.bitwise_xor(from_lane, me), n_dev).astype(F32) + 1.0
        first_half = row_lane < float(half_len)
        for pair in range(n_pair):
            a, b = 2 * pair, 2 * pair + 1
            xa = recv[a, span] * share
            xb = recv[b, span] * share if b < ROWS else jnp.zeros_like(xa)
            parts = _split3(jnp.transpose(jnp.concatenate([xa, xb], axis=0)))
            for j in range(4):
                at = j * n_pair + pair
                for k in range(3):
                    x_ref[h, at, k * n_rows : (k + 1) * n_rows] = parts[k][j * n_rows : (j + 1) * n_rows]
                place_a = by_lane[4 * a + j : 4 * a + j + 1]
                if b < ROWS:
                    place_b = by_lane[4 * b + j : 4 * b + j + 1]
                else:
                    place_a = jnp.where(by_lane[CAP + POOL + j : CAP + POOL + j + 1] == my_bucket, place_a, 0.0)
                    place_b = jnp.zeros_like(place_a)
                wanted = jnp.broadcast_to(jnp.where(first_half, place_a, place_b), (WIDE, LANES)).astype(BF16)
                found_ref[h, at] = jnp.where(vocab == wanted, jnp.ones((), BF16), jnp.zeros((), BF16))
        x = jnp.concatenate([x_ref[h, k] for k in range(4 * n_pair)], axis=1)
        hist = []
        for m in range(2):
            found = jnp.concatenate(
                [found_ref[h, k, m * LANES : (m + 1) * LANES] for k in range(4 * n_pair)], axis=1
            )
            got = lax.dot_general(x, found, (((1,), (1,)), ((), ())), preferred_element_type=F32)
            hist.append(got[:n_rows] + got[n_rows : 2 * n_rows] + got[2 * n_rows :])
        hist = jnp.concatenate(hist, axis=1)
        hists.append(hist)
    peak = functools.reduce(jnp.maximum, peaks)
    shrink = [jnp.exp(p - peak) for p in peaks]
    total = sum(a * b for a, b in zip(shrink, sums))
    lse = peak + jnp.log(total)
    lse_col = jnp.sum(jnp.where(lm_diag, lse, 0.0), axis=1, keepdims=True)
    p_lm = (1.0 - mix_ref[...]) * jnp.exp(logits - lse_col)
    share = mix_ref[...] / total
    p_knn = sum(
        a * jnp.sum(jnp.where(knn_diag, s * share, 0.0), axis=1, keepdims=True) for a, s in zip(hists, shrink)
    )[:, :v_loc]
    if whole:
        outs[0][...] = jnp.log(p_knn + p_lm)
    else:
        outs[0][...] = p_knn
        outs[1][...] = p_lm
    most = jnp.max(jnp.where(row_lane == float(COUNT), peak, 0.0), axis=1, keepdims=True)
    outs[-1][...] = jnp.broadcast_to(most, (1, LANES))

    mine = send.at[:, pl.ds(0, n_dev - 1)]
    pltpu.make_async_copy(mine, mine, send_sem).wait()


def solution(mesh):
    n_dev = mesh.shape["model"]

    def local_step(queries, w_shard, key_shard, tok_shard, temperature, mix_weight):
        n_rows, dim = queries.shape
        n_keys, v_loc = key_shard.shape[0], w_shard.shape[1]
        tok = tok_shard.reshape(n_keys // LANES, LANES)
        any_space = pl.BlockSpec(memory_space=pl.ANY)
        smem = pl.BlockSpec(memory_space=pltpu.SMEM)
        vmem = pl.BlockSpec(memory_space=pltpu.VMEM)
        n_pair = (ROWS + 1) // 2

        def exchange(whole, r):
            block = jax.ShapeDtypeStruct((n_rows, v_loc), F32)
            shapes = [block] if whole else [block, block]
            return pl.pallas_call(
                functools.partial(_kernel, n_dev, whole),
                out_shape=shapes + [jax.ShapeDtypeStruct((1, LANES), F32)],
                in_specs=[smem] + [any_space] * 6,
                out_specs=[vmem] * (len(shapes) + 1),
                scratch_shapes=[
                    pltpu.VMEM((1, 1), F32),
                    pltpu.VMEM((1, 1), F32),
                    pltpu.VMEM((n_rows, dim), BF16),
                    pltpu.VMEM((dim, v_loc), BF16),
                    pltpu.VMEM((dim // LANES, n_keys, LANES), BF16),
                    pltpu.VMEM((n_keys // LANES, LANES), jnp.int32),
                    pltpu.VMEM((n_keys // LANES, n_dev, LANES), BF16),
                    pltpu.VMEM((n_keys // LANES, DEPTH * n_dev + 16, LANES), BF16),
                    pltpu.VMEM((n_keys, LANES), BF16),
                    pltpu.VMEM((6, n_keys, LANES), BF16),
                    pltpu.VMEM((n_keys, LANES), F32),
                    pltpu.VMEM((2, n_keys, LANES), BF16),
                    pltpu.VMEM((n_keys // FINE, 8, LANES), F32),
                    pltpu.VMEM((ROWS + 1, n_dev, LANES), F32),
                    pltpu.VMEM((ROWS + 1, n_dev, LANES), F32),
                    pltpu.VMEM((HALF, 4 * n_pair, 3 * n_rows, LANES), BF16),
                    pltpu.VMEM((HALF, 4 * n_pair, WIDE, LANES), BF16),
                    pltpu.SemaphoreType.DMA((5,)),
                    pltpu.SemaphoreType.DMA((len(CHUNKS),)),
                    pltpu.SemaphoreType.DMA,
                    pltpu.SemaphoreType.DMA((HALF,)),
                ],
                compiler_params=pltpu.CompilerParams(
                    collective_id=0 if whole else 1, has_side_effects=True, vmem_limit_bytes=60 * 1024 * 1024
                ),
            )(r.reshape(1), temperature.reshape(1, 1), mix_weight.reshape(1, 1), queries, w_shard, key_shard, tok)

        out, demand = exchange(True, jnp.int32(0))

        def in_rounds(unused):
            zero = jnp.zeros((n_rows, v_loc), F32)

            def step(carry):
                r, unused, p_knn, unused_lm = carry
                more, p_lm, biggest = exchange(False, r)
                return r + 1, biggest[0, 0], p_knn + more, p_lm

            state = (jnp.int32(0), jnp.float32(1), zero, zero)
            state = lax.while_loop(lambda carry: (carry[0] * CAP).astype(F32) < carry[1], step, state)
            return jnp.log(state[2] + state[3])

        return lax.cond(demand[0, 0] > float(POOL), in_rounds, lambda done: done, out)

    return jax.shard_map(
        local_step,
        mesh=mesh,
        in_specs=(P("data", None), P(None, "model"), P("model", None), P("model"), P(), P()),
        out_specs=P("data", "model"),
        check_vma=False,
    )
```

time: 32.2 us -> 29.8 us (0.925)
  Pallas kernels: 29.3 us -> 26.7 us
    pallas_call x1, Pallas kernels: 29.3 us -> 26.7 us  [exchange(): pl.pallas_call(functools.partial(_kernel, n_dev, whole), out_shape=shapes...]
where the time goes in v3:
time: 29.8 us; the launch traced here: 29.6 us
  Pallas kernels  26.7 us (90%)
  between operations  2.12 us (7%)
  local copies, waits for them, and re-layouts  0.63 us (2%)
    pallas_call x1, Pallas kernels, exchange(): pl.pallas_call(functools.partial(_kernel, n_dev, whole), out_shape=shapes...  26.7 us
    unnamed x7, local copies, waits for them, and re-layouts  0.63 us

profile of v3, /device:TPU:1, one launch (start us, length us, event | category | flops | bytes accessed | tf_op | source)
XLA Modules:
  0.0 29.6 jit_solution(11306329338838047900)
XLA Ops:
  0.0 0.0 copy-start
  0.0 0.0 copy-start.1
  0.0 0.0 copy-start.2
  1.4 26.7 %shard_map.66 = (f32[32,250]{1,0:T(8,128)S(1)}, f32[1,128]{1,0:T(1,128)}) custom-call(s32[1]{0:T(128)} %constant.7.clone.1.rnd_ref, f32[1,1]{1,0:T(1,128)} %bitcast.20.tau_hbm, f32[1,1]{1,0:T(1,128)} %bitcast.21.mix_hbm, bf16[32,2048]{1,0:T(8,128)(2,1)} %q_hbm.1, bf16[2048,250]{1,0:T(8,128)(2,1)} %w_hbm.1, bf16[2048,2048]{1,0:T(8,128)(2,1)} %key_hbm.1, ...), custom_call_target="tpu_custom_call" | custom-call | tf_op jit(solution)/shard_map/pallas_call | solution.py:335
  28.8 0.0 copy-done
  28.8 0.0 copy-done.1
  28.8 0.0 copy-done.2
  28.8 0.2 conditional.1
  29.0 0.6 %copy.30 = f32[32,250]{1,0:T(8,128)} copy(f32[32,250]{1,0:T(8,128)S(1)} %get-tuple-element.86) | data formatting | bytes 64000
Async XLA Ops:
  0.0 28.8 %copy-start = (bf16[2048,250]{1,0:T(8,128)(2,1)S(1)}, bf16[2048,250]{1,0:T(8,128)(2,1)}, u32[]{:S(2)}) copy-start(bf16[2048,250]{1,0:T(8,128)(2,1)} %w_hbm.1) | copy-start | bytes 3072004
  0.0 28.8 %copy-start.1 = (bf16[32,2048]{1,0:T(8,128)(2,1)S(1)}, bf16[32,2048]{1,0:T(8,128)(2,1)}, u32[]{:S(2)}) copy-start(bf16[32,2048]{1,0:T(8,128)(2,1)} %q_hbm.1) | copy-start | bytes 393220
  0.0 28.8 %copy-start.2 = (s32[2048]{0:T(1024)S(1)}, s32[2048]{0:T(1024)}, u32[]{:S(2)}) copy-start(s32[2048]{0:T(1024)} %param.13) | copy-start | bytes 24580

commit v4 on v3

--- a/solution.py
+++ b/solution.py
@@ -14,8 +14,8 @@
 WIDE = 2 * LANES
 DEPTH = 4
 CAP = 8 * DEPTH
-POOL = 4
-ROWS = 2 * DEPTH + 1
+POOL = 8
+ROWS = 2 * DEPTH + 2
 PARTS = 2
 HALF = 2
 COUNT = 48
@@ -226,7 +226,9 @@
                     r * group_len : (r + 1) * group_len, b * LANES : (b + 1) * LANES
                 ]
         if g == 0:
-            send[2 * DEPTH] = jnp.broadcast_to(packed[pool_at : pool_at + 1, :LANES], (n_dev, LANES))
+            for m in range(2):
+                spare = packed[pool_at : pool_at + 1, m * LANES : (m + 1) * LANES]
+                send[2 * DEPTH + m] = jnp.broadcast_to(spare, (n_dev, LANES))
             pl.semaphore_wait(barrier, n_dev - 1)
         for o in range(group_len):
             at = (o * 29 + 29) % group_len
@@ -240,7 +242,7 @@
     recv[:, pl.ds(me, 1), :] = send[:, 0:1, :]
 
     vocab = (_iota((WIDE, LANES), 0) + 1.0).astype(BF16)
-    n_pair = (ROWS + 1) // 2
+    n_pair = ROWS // 2
     peaks, sums, hists = [], [], []
     for h in range(HALF):
         inside = me // half_len == h
@@ -271,18 +273,17 @@
         for pair in range(n_pair):
             a, b = 2 * pair, 2 * pair + 1
             xa = recv[a, span] * share
-            xb = recv[b, span] * share if b < ROWS else jnp.zeros_like(xa)
+            xb = recv[b, span] * share
             parts = _split3(jnp.transpose(jnp.concatenate([xa, xb], axis=0)))
             for j in range(4):
                 at = j * n_pair + pair
                 for k in range(3):
                     x_ref[h, at, k * n_rows : (k + 1) * n_rows] = parts[k][j * n_rows : (j + 1) * n_rows]
                 place_a = by_lane[4 * a + j : 4 * a + j + 1]
-                if b < ROWS:
-                    place_b = by_lane[4 * b + j : 4 * b + j + 1]
-                else:
+                place_b = by_lane[4 * b + j : 4 * b + j + 1]
+                if a == 2 * DEPTH:
                     place_a = jnp.where(by_lane[CAP + POOL + j : CAP + POOL + j + 1] == my_bucket, place_a, 0.0)
-                    place_b = jnp.zeros_like(place_a)
+                    place_b = jnp.where(by_lane[CAP + POOL + 4 + j : CAP + POOL + 5 + j] == my_bucket, place_b, 0.0)
                 wanted = jnp.broadcast_to(jnp.where(first_half, place_a, place_b), (WIDE, LANES)).astype(BF16)
                 found_ref[h, at] = jnp.where(vocab == wanted, jnp.ones((), BF16), jnp.zeros((), BF16))
         x = jnp.concatenate([x_ref[h, k] for k in range(4 * n_pair)], axis=1)
@@ -327,7 +328,7 @@
         any_space = pl.BlockSpec(memory_space=pl.ANY)
         smem = pl.BlockSpec(memory_space=pltpu.SMEM)
         vmem = pl.BlockSpec(memory_space=pltpu.VMEM)
-        n_pair = (ROWS + 1) // 2
+        n_pair = ROWS // 2
 
         def exchange(whole, r):
             block = jax.ShapeDtypeStruct((n_rows, v_loc), F32)

time: 29.8 us -> 30.4 us (1.020)
  Pallas kernels: 26.7 us -> 27.4 us
    pallas_call x1, Pallas kernels: 26.7 us -> 27.4 us  [exchange(): pl.pallas_call(functools.partial(_kernel, n_dev, whole), out_shape=shapes...]
where the time goes in v4:
time: 30.4 us; the launch traced here: 30.3 us
  Pallas kernels  27.4 us (90%)
  between operations  2.12 us (7%)
  local copies, waits for them, and re-layouts  0.63 us (2%)
    pallas_call x1, Pallas kernels, exchange(): pl.pallas_call(functools.partial(_kernel, n_dev, whole), out_shape=shapes...  27.4 us
    unnamed x7, local copies, waits for them, and re-layouts  0.63 us

profile of v4, /device:TPU:1, one launch (start us, length us, event | category | flops | bytes accessed | tf_op | source)
XLA Modules:
  0.0 30.3 jit_solution(13353479806172742790)
XLA Ops:
  0.0 0.0 copy-start
  0.0 0.0 copy-start.1
  0.0 0.0 copy-start.2
  1.4 27.4 %shard_map.66 = (f32[32,250]{1,0:T(8,128)S(1)}, f32[1,128]{1,0:T(1,128)}) custom-call(s32[1]{0:T(128)} %constant.7.clone.1.rnd_ref, f32[1,1]{1,0:T(1,128)} %bitcast.20.tau_hbm, f32[1,1]{1,0:T(1,128)} %bitcast.21.mix_hbm, bf16[32,2048]{1,0:T(8,128)(2,1)} %q_hbm.1, bf16[2048,250]{1,0:T(8,128)(2,1)} %w_hbm.1, bf16[2048,2048]{1,0:T(8,128)(2,1)} %key_hbm.1, ...), custom_call_target="tpu_custom_call" | custom-call | tf_op jit(solution)/shard_map/pallas_call | solution.py:336
  29.5 0.0 copy-done
  29.5 0.0 copy-done.1
  29.5 0.0 copy-done.2
  29.5 0.2 conditional.1
  29.7 0.6 %copy.30 = f32[32,250]{1,0:T(8,128)} copy(f32[32,250]{1,0:T(8,128)S(1)} %get-tuple-element.86) | data formatting | bytes 64000
Async XLA Ops:
  0.0 29.5 %copy-start = (bf16[2048,250]{1,0:T(8,128)(2,1)S(1)}, bf16[2048,250]{1,0:T(8,128)(2,1)}, u32[]{:S(2)}) copy-start(bf16[2048,250]{1,0:T(8,128)(2,1)} %w_hbm.1) | copy-start | bytes 3072004
  0.0 29.5 %copy-start.1 = (bf16[32,2048]{1,0:T(8,128)(2,1)S(1)}, bf16[32,2048]{1,0:T(8,128)(2,1)}, u32[]{:S(2)}) copy-start(bf16[32,2048]{1,0:T(8,128)(2,1)} %q_hbm.1) | copy-start | bytes 393220
  0.0 29.5 %copy-start.2 = (s32[2048]{0:T(1024)S(1)}, s32[2048]{0:T(1024)}, u32[]{:S(2)}) copy-start(s32[2048]{0:T(1024)} %param.13) | copy-start | bytes 24580

commit v5 on v4

--- a/solution.py
+++ b/solution.py
@@ -16,14 +16,14 @@
 CAP = 8 * DEPTH
 POOL = 8
 ROWS = 2 * DEPTH + 2
-PARTS = 2
+PARTS = 4
 HALF = 2
 COUNT = 48
 STAT = 64
 EMPTY = 255.0
 CHUNKS = (512, 512, 512, 512)
 SORTED = (8, 12, 16, 16)
-FINE = 256
+FINE = 64
 
 
 def _iota(shape, dim):
@@ -346,7 +346,7 @@
                     pltpu.VMEM((dim // LANES, n_keys, LANES), BF16),
                     pltpu.VMEM((n_keys // LANES, LANES), jnp.int32),
                     pltpu.VMEM((n_keys // LANES, n_dev, LANES), BF16),
-                    pltpu.VMEM((n_keys // LANES, DEPTH * n_dev + 16, LANES), BF16),
+                    pltpu.VMEM((n_keys // LANES, DEPTH * n_dev + 16 * (PARTS - 1), LANES), BF16),
                     pltpu.VMEM((n_keys, LANES), BF16),
                     pltpu.VMEM((6, n_keys, LANES), BF16),
                     pltpu.VMEM((n_keys, LANES), F32),

time: 30.4 us -> 29.1 us (0.957)
  Pallas kernels: 27.4 us -> 26 us
    pallas_call x1, Pallas kernels: 27.4 us -> 26 us  [exchange(): pl.pallas_call(functools.partial(_kernel, n_dev, whole), out_shape=shapes...]
where the time goes in v5:
time: 29.1 us; the launch traced here: 29 us
  Pallas kernels  26 us (89%)
  between operations  2.12 us (7%)
  local copies, waits for them, and re-layouts  0.63 us (2%)
    pallas_call x1, Pallas kernels, exchange(): pl.pallas_call(functools.partial(_kernel, n_dev, whole), out_shape=shapes...  26 us
    unnamed x7, local copies, waits for them, and re-layouts  0.63 us

profile of v5, /device:TPU:1, one launch (start us, length us, event | category | flops | bytes accessed | tf_op | source)
XLA Modules:
  0.0 29.0 jit_solution(13962458849328036536)
XLA Ops:
  0.0 0.0 copy-start
  0.0 0.0 copy-start.1
  0.0 0.0 copy-start.2
  1.4 26.0 %shard_map.66 = (f32[32,250]{1,0:T(8,128)S(1)}, f32[1,128]{1,0:T(1,128)}) custom-call(s32[1]{0:T(128)} %constant.7.clone.1.rnd_ref, f32[1,1]{1,0:T(1,128)} %bitcast.20.tau_hbm, f32[1,1]{1,0:T(1,128)} %bitcast.21.mix_hbm, bf16[32,2048]{1,0:T(8,128)(2,1)} %q_hbm.1, bf16[2048,250]{1,0:T(8,128)(2,1)} %w_hbm.1, bf16[2048,2048]{1,0:T(8,128)(2,1)} %key_hbm.1, ...), custom_call_target="tpu_custom_call" | custom-call | tf_op jit(solution)/shard_map/pallas_call | solution.py:336
  28.1 0.0 copy-done
  28.1 0.0 copy-done.1
  28.2 0.0 copy-done.2
  28.2 0.2 conditional.1
  28.4 0.6 %copy.30 = f32[32,250]{1,0:T(8,128)} copy(f32[32,250]{1,0:T(8,128)S(1)} %get-tuple-element.86) | data formatting | bytes 64000
Async XLA Ops:
  0.0 28.1 %copy-start = (bf16[2048,250]{1,0:T(8,128)(2,1)S(1)}, bf16[2048,250]{1,0:T(8,128)(2,1)}, u32[]{:S(2)}) copy-start(bf16[2048,250]{1,0:T(8,128)(2,1)} %w_hbm.1) | copy-start | bytes 3072004
  0.0 28.1 %copy-start.1 = (bf16[32,2048]{1,0:T(8,128)(2,1)S(1)}, bf16[32,2048]{1,0:T(8,128)(2,1)}, u32[]{:S(2)}) copy-start(bf16[32,2048]{1,0:T(8,128)(2,1)} %q_hbm.1) | copy-start | bytes 393220
  0.0 28.2 %copy-start.2 = (s32[2048]{0:T(1024)S(1)}, s32[2048]{0:T(1024)}, u32[]{:S(2)}) copy-start(s32[2048]{0:T(1024)} %param.13) | copy-start | bytes 24580
